TPU v7x, 256 devices: a whole 4x4x8 slice. The times are simulated.
256 devices in a mesh: ep: 32 (over x, z), tp: 8 (over y, core).
Axes of the slice: x: 4, y: 4, z: 8, core: 2. Of those that a mesh axis runs over, the one named last changes fastest.
Arguments:
- tokens: bfloat16 [8192, 2880], P('ep', 'tp'), may hold values from -6 to 6
- expert_ids: int32 [8192, 4], P('ep'), may hold values from 0 to 63, all different within a row; in each aligned block of 256 rows (0 to 255, 256 to 511, ...) at most 32 rows name the same one
- combine_weights: float32 [8192, 4], P('ep'), may hold values from 0.05 to 0.6
- gate_weight: bfloat16 [64, 2880, 2880], P('ep', None, 'tp'), may hold values from -0.109375 to 0.109375
- up_weight: bfloat16 [64, 2880, 2880], P('ep', None, 'tp'), may hold values from -0.109375 to 0.109375
- down_weight: bfloat16 [64, 2880, 2880], P('ep', 'tp'), may hold values from -0.109375 to 0.109375
Outputs:
- mixed: bfloat16 [8192, 2880], P('ep', 'tp')
Inputs may be any that keep to these rules, and one draw needn't show every extreme that they name: `expert_ids`: each row names 4 different experts; within the 256 rows of one index of ep no expert is named more than 32 times, a bound that some block reaches.
All inputs are finite; a program needn't handle non-finite values.
Results may differ from a plain program's by a relative error of at most 0.014.
Values may be sent and summed in bfloat16 or wider, within the bound.
No kernel may reach another device: no remote copies, remote signals or barrier semaphores. Data moves between devices by JAX's collectives and lax.ppermute only.
A program may use at most 128 MiB of HBM per device.

v0:
```python
import jax
import jax.numpy as jnp
from jax import lax
from jax.sharding import Mesh
from jax.sharding import PartitionSpec as P

TP = ("tp_0", "tp_1")


def reduced_to_own(pieces, axes, sequence):
    inside = pieces.shape[1:]
    pieces = pieces.reshape(*(lax.axis_size(a) for a in axes), *inside)
    pieces = jnp.moveaxis(pieces, sequence, range(len(axes))).reshape(-1, *inside)
    for k in sequence:
        pieces = lax.psum_scatter(pieces, axes[k], scatter_dimension=0, tiled=True)
    return pieces[0]


def split_up(array, dim, count):
    before, after = (array.shape[:dim], array.shape[dim + 1 :])
    return jnp.moveaxis(array.reshape(*before, count, -1, *after), dim, 0)


def scatter_axes(array, axes, sequence, dim):
    count = lax.axis_size(axes)
    return reduced_to_own(split_up(array, dim, count), axes, sequence)


def activate(gate_acc, up_acc):
    return (up_acc + 1.0) * gate_acc * jax.nn.sigmoid(1.702 * gate_acc)


def local(tokens, expert_ids, combine_weights, gate_weight, up_weight, down_weight):
    ep_count = lax.axis_size("ep")
    exp_local = gate_weight.shape[0]
    experts = exp_local * ep_count
    tok_rows = expert_ids.shape[0]
    top_count = expert_ids.shape[1]
    capacity = 2 * tok_rows * top_count // experts
    feat_width = tokens.shape[1]
    flat_ids = expert_ids.reshape(-1)
    onehot = (flat_ids[:, None] == jnp.arange(experts, dtype=jnp.int32)[None, :]).astype(jnp.int32)
    slot_pos = jnp.sum((jnp.cumsum(onehot, axis=0) - onehot) * onehot, axis=1)
    expert_local = flat_ids % exp_local
    owner_dev = flat_ids // exp_local
    token_of = jnp.arange(tok_rows * top_count, dtype=jnp.int32) // top_count
    send_buf = jnp.zeros((exp_local, ep_count, capacity, feat_width), jnp.bfloat16)
    send_buf = send_buf.at[expert_local, owner_dev, slot_pos].set(tokens[token_of])
    arrived = lax.all_to_all(send_buf, "ep", split_axis=1, concat_axis=1, tiled=True)
    arrived = arrived.reshape(exp_local, ep_count * capacity, feat_width)
    shard_piece = lax.all_gather(arrived, TP, axis=2, tiled=True)
    gate_new = jnp.einsum(
        "erd,edf->erf", shard_piece, gate_weight, preferred_element_type=jnp.float32
    )
    up_new = jnp.einsum("erd,edf->erf", shard_piece, up_weight, preferred_element_type=jnp.float32)
    hidden = activate(gate_new, up_new).astype(jnp.bfloat16)
    partials = jnp.einsum("erf,efd->erd", hidden, down_weight, preferred_element_type=jnp.float32)
    weights_flat = combine_weights.reshape(-1)
    summed = scatter_axes(partials.astype(jnp.bfloat16), TP, (1, 0), 2).astype(jnp.float32)
    summed = summed.reshape(exp_local, ep_count, capacity, summed.shape[2])
    returned = lax.all_to_all(
        summed.astype(jnp.bfloat16), "ep", split_axis=1, concat_axis=1, tiled=True
    ).astype(summed.dtype)
    picked = returned[expert_local, owner_dev, slot_pos]
    weighted = (picked * weights_flat[:, None]).reshape(tok_rows, top_count, picked.shape[1])
    mixed = jnp.sum(weighted, axis=1).astype(jnp.bfloat16)
    return mixed


def solution(mesh):
    split = Mesh(mesh.devices.reshape(mesh.shape["ep"], 4, 2), ("ep", "tp_0", "tp_1"))
    placed = (
        P("ep", TP),
        P("ep", None),
        P("ep", None),
        P("ep", None, TP),
        P("ep", None, TP),
        P("ep", TP, None),
    )
    return jax.shard_map(local, mesh=split, in_specs=placed, out_specs=P("ep", TP), check_vma=False)
```

profile of v0, /device:TPU:32, one launch (start us, length us, event | category | flops | bytes accessed | tf_op | source)
XLA Modules:
  0.0 360.9 jit_solution(3638396333141942187)
XLA Ops:
  6.5 0.9 copy.61
  7.8 18.0 %reduce-window.6 = s32[64,8,128]{2,1,0:T(8,128)S(1)} reduce-window(s32[64,8,128]{2,1,0:T(8,128)S(1)} %fusion.6, s32[]{:T(128)} %constant.47.clone.1), window={size=1x1x128 pad=0_0x0_0x127_0}, to_apply=%region_0.0 | reduce-window | flops 8323072 | bytes 524292 | tf_op jit(solution)/shard_map/reduce-window
  26.7 0.2 copy.66
  26.9 9.4 %scatter_custom_fusion = bf16[2048,360]{1,0:T(8,128)(2,1)S(1)} fusion(s32[1024]{0:T(1024)S(1)} %get-tuple-element.10, bf16[256,360]{1,0:T(8,128)(2,1)S(1)} %copy.66, s32[1024]{0:T(1024)S(1)} %get-tuple-element.9, bf16[]{:T(256)} %constant.46.clone.1), kind=kCustom, calls=%fused_computation.7 | custom fusion | bytes 1474562
  36.3 0.3 copy.67
  36.6 51.1 %all_to_all.10 = bf16[2,32,32,360]{3,2,0,1:T(8,128)(2,1)S(1)} all-to-all(bf16[2,32,32,360]{3,2,0,1:T(8,128)(2,1)S(1)} %copy.67), channel_id=1, replica_groups=mesh['ep'=32,'tp_0'=4,'tp_1'=2] {'ep'}, dimensions={1} | all-to-all | bytes 2949120 | tf_op jit(solution)/shard_map/all_to_all | solution.py:49
  87.6 0.2 copy.68
  87.8 1.6 copy.69
  89.5 0.2 reduce-scatter.3.cloned.1.call-start
  89.7 62.7 %all-gather.2.cloned.1.call-done = bf16[2,1024,2880]{1,2,0:T(8,128)(2,1)} async-done(((bf16[2,1024,360]{1,2,0:T(8,128)(2,1)}), bf16[2,1024,2880]{1,2,0:T(8,128)(2,1)}) %all-gather.2.cloned.1.call-update) | async-done | bytes 11796496 | tf_op jit(solution)/shard_map/all_gather | solution.py:51
  152.4 8.8 %fusion.7 = f32[2,1024,360]{1,2,0:T(8,128)S(1)} fusion(bf16[2,1024,2880]{1,2,0:T(8,128)(2,1)} %all-gather.2.cloned.1.call-done, bf16[2,2880,360]{1,2,0:T(8,128)(2,1)} %param.9), kind=kOutput, calls=%fused_computation.37 | convolution fusion | flops 4246732800 | bytes 18892800 | tf_op jit(solution)/shard_map/erd,edf->erf/dot_general | solution.py:52
  161.3 18.4 %convolution_convert_fusion = bf16[2,1024,2880]{1,2,0:T(8,128)(2,1)} fusion(bf16[2,360,2880]{2,1,0:T(8,128)(2,1)} %param.11, f32[2,1024,360]{1,2,0:T(8,128)S(1)} %fusion.7, bf16[2,1024,2880]{1,2,0:T(8,128)(2,1)} %all-gather.2.cloned.1.call-done, bf16[2,2880,360]{1,2,0:T(8,128)(2,1)} %param.10), kind=kOutput, calls=%fused_computation.3 | convolution fusion | flops 8505262080 | bytes 34836480 | tf_op jit(solution)/shard_map/erf,efd->erd/dot_general | solution.py:57
  179.7 10.2 %copy.71 = bf16[2,4,2,1024,360]{3,4,2,1,0:T(8,128)(2,1)} copy(bf16[2,4,2,1024,360]{3,4,0,1,2:T(8,128)(2,1)} %bitcast.47) | data formatting | bytes 23592960 | tf_op jit(solution)/shard_map/transpose | solution.py:13
  190.0 26.8 %reduce-scatter.3.cloned.1.call-done = bf16[4,2,1024,360]{2,3,1,0:T(8,128)(2,1)} async-done(((bf16[8,2,1024,360]{2,3,1,0:T(8,128)(2,1)}), bf16[4,2,1024,360]{2,3,1,0:T(8,128)(2,1)}) %reduce-scatter.3.cloned.1.call-update) | async-done | bytes 5898256 | tf_op jit(solution)/shard_map/reduce_scatter | solution.py:15
  216.8 65.4 %reduce-scatter.5.cloned.1.call-done = bf16[1,2,1024,360]{2,3,1,0:T(8,128)(2,1)} async-done(((bf16[4,2,1024,360]{2,3,1,0:T(8,128)(2,1)}), bf16[1,2,1024,360]{2,3,1,0:T(8,128)(2,1)}) %reduce-scatter.5.cloned.1.call-update) | async-done | bytes 1474576 | tf_op jit(solution)/shard_map/reduce_scatter | solution.py:15
  282.2 1.8 copy.72
  284.1 1.4 copy.73
  285.5 10.1 %all-to-all-start.1 = ((bf16[2,32,32,360]{3,2,0,1:T(8,128)(2,1)}), bf16[2,32,32,360]{3,2,0,1:T(8,128)(2,1)}, u32[]{:S(2)}, u32[]{:S(2)}) async-start(bf16[2,32,32,360]{3,2,0,1:T(8,128)(2,1)} %copy.73), calls=%async_computation.3 | async-start | bytes 3145728 | tf_op jit(solution)/shard_map/all_to_all | solution.py:61
  295.8 39.0 %all-to-all-done.1 = bf16[2,32,32,360]{3,2,0,1:T(8,128)(2,1)} async-done(((bf16[2,32,32,360]{3,2,0,1:T(8,128)(2,1)}), bf16[2,32,32,360]{3,2,0,1:T(8,128)(2,1)}, u32[]{:S(2)}, u32[]{:S(2)}) %all-to-all-start.1) | async-done | bytes 1474592 | tf_op jit(solution)/shard_map/all_to_all | solution.py:61
  334.8 1.8 copy_convert_fusion
  336.6 14.1 %gather_fusion = f32[1024,360]{1,0:T(8,128)} fusion(f32[2,32,32,360]{3,2,1,0:T(8,128)S(1)} %copy_convert_fusion, s32[1024]{0:T(1024)S(1)} %bitcast.45), kind=kCustom, calls=%fused_computation.1 | custom fusion | bytes 2961408 | tf_op jit(solution)/shard_map/gather | solution.py:64
  350.7 1.8 gather.10
  352.5 1.0 multiply_reduce_fusion
  353.5 0.8 copy.76
  (30 shorter events, 1.5 us)
Async XLA Ops:
  6.5 20.0 %copy-start.3 = (s32[3]{0:T(128)S(1)}, s32[3]{0:T(128)}, u32[]{:S(2)}) copy-start(s32[3]{0:T(128)} %constant.60) | copy-start | bytes 40
  6.5 20.1 %copy-start.2 = (s32[3]{0:T(128)S(1)}, s32[3]{0:T(128)}, u32[]{:S(2)}) copy-start(s32[3]{0:T(128)} %constant.63) | copy-start | bytes 40
  6.5 20.2 %copy-start = (bf16[256,360]{0,1:T(8,128)(2,1)S(1)}, bf16[256,360]{0,1:T(8,128)(2,1)}, u32[]{:S(2)}) copy-start(bf16[256,360]{0,1:T(8,128)(2,1)} %param.6) | copy-start | bytes 552964
  6.5 145.9 %all-gather.2.cloned.1.call-start = ((), (), s32[]{:S(2)}) async-start(), calls=%async_computation.4 | async-start | bytes 13271040 | tf_op jit(solution)/shard_map/all_gather | solution.py:51
  89.5 127.3 %reduce-scatter.3.cloned.1.call-start = ((), (), s32[]{:S(2)}) async-start(), calls=%async_computation.5 | async-start | bytes 17694720 | tf_op jit(solution)/shard_map/reduce_scatter | solution.py:15
  190.0 92.3 %reduce-scatter.5.cloned.1.call-start = ((), (), s32[]{:S(2)}) async-start(), calls=%async_computation.6 | async-start | bytes 7372800 | tf_op jit(solution)/shard_map/reduce_scatter | solution.py:15
  284.1 11.5 %copy-start.1 = (f32[256,4]{0,1:T(4,128)S(1)}, f32[256,4]{0,1:T(4,128)}, u32[]{:S(2)}) copy-start(f32[256,4]{0,1:T(4,128)} %param.8) | copy-start | bytes 12292
  285.5 49.3 %all-to-all-start.1 = ((bf16[2,32,32,360]{3,2,0,1:T(8,128)(2,1)}), bf16[2,32,32,360]{3,2,0,1:T(8,128)(2,1)}, u32[]{:S(2)}, u32[]{:S(2)}) async-start(bf16[2,32,32,360]{3,2,0,1:T(8,128)(2,1)} %copy.73), calls=%async_computation.3 | async-start | bytes 3145728 | tf_op jit(solution)/shard_map/all_to_all | solution.py:61
Sparse Core Ops, SparseCore 0:
  89.6 62.7 all-gather.1
  190.1 26.6 reduce-scatter.2
  219.4 62.7 reduce-scatter.4
where the time goes:
time: 361 us
  waiting for transfers between devices  194 us (54%)
  blocking collectives  51.1 us (14%)
  local copies, waits for them, and re-layouts  43.5 us (12%)
  matrix products  27.3 us (8%)
  other arithmetic  21.4 us (6%)
  between operations  13.3 us (4%)
  starting transfers between devices  10.4 us (3%)
    reduce_scatter x2, waiting for transfers between devices, reduced_to_own(): pieces = lax.psum_scatter(pieces, axes[k], scatter_dimension=0, tiled=True)  92.2 us
    all_gather x1, waiting for transfers between devices, local(): shard_piece = lax.all_gather(arrived, TP, axis=2, tiled=True)  62.7 us
    all_to_all x1, blocking collectives, local(): lax.all_to_all(send_buf, 'ep', split_axis=1, concat_axis=1, tiled=True)  51.1 us
    all_to_all x1, waiting for transfers between devices, local(): lax.all_to_all(summed.astype(jnp.bfloat16), 'ep', split_axis=1, concat_ax...  39 us
    dot_general x1, matrix products, local(): jnp.einsum('erf,efd->erd', hidden, down_weight, preferred_element_type=jn...  18.4 us
    another operation x3, other arithmetic  18.2 us
    gather x2, local copies, waits for them, and re-layouts, local(): picked = returned[expert_local, owner_dev, slot_pos]  15.9 us
    unnamed x12, local copies, waits for them, and re-layouts  10.5 us
  transfers between devices with their start and end apart: 4, of which 4 were waited for; matrix products, arithmetic and copies ran while one was open for 0% of the time, Pallas kernels for 0%

commit v1 on v0

--- a/solution.py
+++ b/solution.py
@@ -48,7 +48,7 @@
     send_buf = send_buf.at[expert_local, owner_dev, slot_pos].set(tokens[token_of])
     arrived = lax.all_to_all(send_buf, "ep", split_axis=1, concat_axis=1, tiled=True)
     arrived = arrived.reshape(exp_local, ep_count * capacity, feat_width)
-    shard_piece = lax.all_gather(arrived, TP, axis=2, tiled=True)
+    shard_piece = jnp.concatenate(lax.all_gather(arrived, TP), axis=2)
     gate_new = jnp.einsum(
         "erd,edf->erf", shard_piece, gate_weight, preferred_element_type=jnp.float32
     )

time: 361 us -> 372 us (1.030)
  local copies, waits for them, and re-layouts: 43.5 us -> 53.7 us
    reshape x1, local copies, waits for them, and re-layouts: 1.63 us -> 10.1 us  [local(): shard_piece = jnp.concatenate(lax.all_gather(arrived, TP), axis=2)]
where the time goes in v1:
time: 372 us; the launch traced here: 371 us
  waiting for transfers between devices  194 us (52%)
  local copies, waits for them, and re-layouts  53.7 us (14%)
  blocking collectives  51.1 us (14%)
  matrix products  27.3 us (7%)
  other arithmetic  21.4 us (6%)
  between operations  13.3 us (4%)
  starting transfers between devices  10.4 us (3%)
    reduce_scatter x2, waiting for transfers between devices, reduced_to_own(): pieces = lax.psum_scatter(pieces, axes[k], scatter_dimension=0, tiled=True)  92.5 us
    all_gather x1, waiting for transfers between devices, local(): shard_piece = jnp.concatenate(lax.all_gather(arrived, TP), axis=2)  62.7 us
    all_to_all x1, blocking collectives, local(): lax.all_to_all(send_buf, 'ep', split_axis=1, concat_axis=1, tiled=True)  51.1 us
    all_to_all x1, waiting for transfers between devices, local(): lax.all_to_all(summed.astype(jnp.bfloat16), 'ep', split_axis=1, concat_ax...  39 us
    dot_general x1, matrix products, local(): jnp.einsum('erf,efd->erd', hidden, down_weight, preferred_element_type=jn...  18.4 us
    another operation x3, other arithmetic  18.2 us
    gather x2, local copies, waits for them, and re-layouts, local(): picked = returned[expert_local, owner_dev, slot_pos]  15.9 us
    unnamed x12, local copies, waits for them, and re-layouts  10.5 us
  transfers between devices with their start and end apart: 4, of which 4 were waited for; matrix products, arithmetic and copies ran while one was open for 0% of the time, Pallas kernels for 0%

profile of v1, /device:TPU:32, one launch (start us, length us, event | category | flops | bytes accessed | tf_op | source)
XLA Modules:
  0.0 371.4 jit_solution(14187660136352492603)
XLA Ops:
  6.5 0.9 copy.64
  7.8 18.0 %reduce-window.6 = s32[64,8,128]{2,1,0:T(8,128)S(1)} reduce-window(s32[64,8,128]{2,1,0:T(8,128)S(1)} %fusion.6, s32[]{:T(128)} %constant.47.clone.1), window={size=1x1x128 pad=0_0x0_0x127_0}, to_apply=%region_0.0 | reduce-window | flops 8323072 | bytes 524292 | tf_op jit(solution)/shard_map/reduce-window
  26.7 0.2 copy.69
  26.9 9.4 %scatter_custom_fusion = bf16[2048,360]{1,0:T(8,128)(2,1)S(1)} fusion(s32[1024]{0:T(1024)S(1)} %get-tuple-element.10, bf16[256,360]{1,0:T(8,128)(2,1)S(1)} %copy.69, s32[1024]{0:T(1024)S(1)} %get-tuple-element.9, bf16[]{:T(256)} %constant.46.clone.1), kind=kCustom, calls=%fused_computation.7 | custom fusion | bytes 1474562
  36.3 0.3 copy.70
  36.6 51.1 %all_to_all.10 = bf16[2,32,32,360]{3,2,0,1:T(8,128)(2,1)S(1)} all-to-all(bf16[2,32,32,360]{3,2,0,1:T(8,128)(2,1)S(1)} %copy.70), channel_id=1, replica_groups=mesh['ep'=32,'tp_0'=4,'tp_1'=2] {'ep'}, dimensions={1} | all-to-all | bytes 2949120 | tf_op jit(solution)/shard_map/all_to_all | solution.py:49
  87.8 1.6 copy.72
  89.5 0.2 reduce-scatter.3.cloned.1.call-start
  89.7 62.7 %all-gather.2.cloned.1.call-done = bf16[8,2,1024,360]{2,3,1,0:T(8,128)(2,1)} async-done(((bf16[1,2,1024,360]{2,3,1,0:T(8,128)(2,1)}), bf16[8,2,1024,360]{2,3,1,0:T(8,128)(2,1)}) %all-gather.2.cloned.1.call-update) | async-done | bytes 11796496 | tf_op jit(solution)/shard_map/all_gather | solution.py:51
  152.4 10.1 %copy.73 = bf16[2,1024,8,360]{1,3,2,0:T(8,128)(2,1)} copy(bf16[2,1024,8,360]{1,3,0,2:T(8,128)(2,1)} %bitcast.49) | data formatting | bytes 23592960 | tf_op jit(solution)/shard_map/reshape | solution.py:51
  162.6 8.8 %fusion.7 = f32[2,1024,360]{1,2,0:T(8,128)S(1)} fusion(bf16[2,1024,2880]{1,2,0:T(8,128)(2,1)} %bitcast.50, bf16[2,2880,360]{1,2,0:T(8,128)(2,1)} %param.9), kind=kOutput, calls=%fused_computation.37 | convolution fusion | flops 4246732800 | bytes 18892800 | tf_op jit(solution)/shard_map/erd,edf->erf/dot_general | solution.py:52
  171.4 18.4 %convolution_convert_fusion = bf16[2,1024,2880]{1,2,0:T(8,128)(2,1)} fusion(bf16[2,360,2880]{2,1,0:T(8,128)(2,1)} %param.11, f32[2,1024,360]{1,2,0:T(8,128)S(1)} %fusion.7, bf16[2,1024,2880]{1,2,0:T(8,128)(2,1)} %bitcast.51, bf16[2,2880,360]{1,2,0:T(8,128)(2,1)} %param.10), kind=kOutput, calls=%fused_computation.3 | convolution fusion | flops 8505262080 | bytes 34836480 | tf_op jit(solution)/shard_map/erf,efd->erd/dot_general | solution.py:57
  189.8 10.2 %copy.75 = bf16[2,4,2,1024,360]{3,4,2,1,0:T(8,128)(2,1)} copy(bf16[2,4,2,1024,360]{3,4,0,1,2:T(8,128)(2,1)} %bitcast.52) | data formatting | bytes 23592960 | tf_op jit(solution)/shard_map/transpose | solution.py:13
  200.2 26.8 %reduce-scatter.3.cloned.1.call-done = bf16[4,2,1024,360]{2,3,1,0:T(8,128)(2,1)} async-done(((bf16[8,2,1024,360]{2,3,1,0:T(8,128)(2,1)}), bf16[4,2,1024,360]{2,3,1,0:T(8,128)(2,1)}) %reduce-scatter.3.cloned.1.call-update) | async-done | bytes 5898256 | tf_op jit(solution)/shard_map/reduce_scatter | solution.py:15
  227.0 65.7 %reduce-scatter.5.cloned.1.call-done = bf16[1,2,1024,360]{2,3,1,0:T(8,128)(2,1)} async-done(((bf16[4,2,1024,360]{2,3,1,0:T(8,128)(2,1)}), bf16[1,2,1024,360]{2,3,1,0:T(8,128)(2,1)}) %reduce-scatter.5.cloned.1.call-update) | async-done | bytes 1474576 | tf_op jit(solution)/shard_map/reduce_scatter | solution.py:15
  292.7 1.9 copy.76
  294.5 1.5 copy.77
  296.0 10.1 %all-to-all-start.1 = ((bf16[2,32,32,360]{3,2,0,1:T(8,128)(2,1)}), bf16[2,32,32,360]{3,2,0,1:T(8,128)(2,1)}, u32[]{:S(2)}, u32[]{:S(2)}) async-start(bf16[2,32,32,360]{3,2,0,1:T(8,128)(2,1)} %copy.77), calls=%async_computation.3 | async-start | bytes 3145728 | tf_op jit(solution)/shard_map/all_to_all | solution.py:61
  306.2 39.0 %all-to-all-done.1 = bf16[2,32,32,360]{3,2,0,1:T(8,128)(2,1)} async-done(((bf16[2,32,32,360]{3,2,0,1:T(8,128)(2,1)}), bf16[2,32,32,360]{3,2,0,1:T(8,128)(2,1)}, u32[]{:S(2)}, u32[]{:S(2)}) %all-to-all-start.1) | async-done | bytes 1474592 | tf_op jit(solution)/shard_map/all_to_all | solution.py:61
  345.2 1.8 copy_convert_fusion
  347.1 14.1 %gather_fusion = f32[1024,360]{1,0:T(8,128)} fusion(f32[2,32,32,360]{3,2,1,0:T(8,128)S(1)} %copy_convert_fusion, s32[1024]{0:T(1024)S(1)} %bitcast.47), kind=kCustom, calls=%fused_computation.1 | custom fusion | bytes 2961408 | tf_op jit(solution)/shard_map/gather | solution.py:64
  361.2 1.8 gather.10
  363.0 1.0 multiply_reduce_fusion
  364.0 0.8 copy.80
  (31 shorter events, 1.6 us)
Async XLA Ops:
  6.5 20.0 %copy-start.3 = (s32[3]{0:T(128)S(1)}, s32[3]{0:T(128)}, u32[]{:S(2)}) copy-start(s32[3]{0:T(128)} %constant.60) | copy-start | bytes 40
  6.5 20.1 %copy-start.2 = (s32[3]{0:T(128)S(1)}, s32[3]{0:T(128)}, u32[]{:S(2)}) copy-start(s32[3]{0:T(128)} %constant.63) | copy-start | bytes 40
  6.5 20.2 %copy-start = (bf16[256,360]{0,1:T(8,128)(2,1)S(1)}, bf16[256,360]{0,1:T(8,128)(2,1)}, u32[]{:S(2)}) copy-start(bf16[256,360]{0,1:T(8,128)(2,1)} %param.6) | copy-start | bytes 552964
  6.5 145.9 %all-gather.2.cloned.1.call-start = ((), (), s32[]{:S(2)}) async-start(), calls=%async_computation.4 | async-start | bytes 13271040 | tf_op jit(solution)/shard_map/all_gather | solution.py:51
  89.5 137.5 %reduce-scatter.3.cloned.1.call-start = ((), (), s32[]{:S(2)}) async-start(), calls=%async_computation.5 | async-start | bytes 17694720 | tf_op jit(solution)/shard_map/reduce_scatter | solution.py:15
  200.1 92.5 %reduce-scatter.5.cloned.1.call-start = ((), (), s32[]{:S(2)}) async-start(), calls=%async_computation.6 | async-start | bytes 7372800 | tf_op jit(solution)/shard_map/reduce_scatter | solution.py:15
  294.5 11.6 %copy-start.1 = (f32[256,4]{0,1:T(4,128)S(1)}, f32[256,4]{0,1:T(4,128)}, u32[]{:S(2)}) copy-start(f32[256,4]{0,1:T(4,128)} %param.8) | copy-start | bytes 12292
  296.0 49.3 %all-to-all-start.1 = ((bf16[2,32,32,360]{3,2,0,1:T(8,128)(2,1)}), bf16[2,32,32,360]{3,2,0,1:T(8,128)(2,1)}, u32[]{:S(2)}, u32[]{:S(2)}) async-start(bf16[2,32,32,360]{3,2,0,1:T(8,128)(2,1)} %copy.77), calls=%async_computation.3 | async-start | bytes 3145728 | tf_op jit(solution)/shard_map/all_to_all | solution.py:61
Sparse Core Ops, SparseCore 0:
  89.6 62.7 all-gather.1
  200.2 26.6 reduce-scatter.2
  229.5 63.0 reduce-scatter.4
